TPU v7x, 32 devices: a whole 2x2x4 slice. The times are simulated.
32 devices in a mesh: groups: 2 (over y), expert: 4 (over x, core), tensor: 4 (over z).
Axes of the slice: x: 2, y: 2, z: 4, core: 2. Of those that a mesh axis runs over, the one named last changes fastest.
Arguments:
- tokens: bfloat16 [512, 4096], P(('groups', 'expert'), 'tensor'), parts along dimension 0, may hold values from -400 to 400
- norm_gain: float32 [4096], replicated, may hold values from 0.5 to 1.5
- w_gate: bfloat16 [4096, 65536], P(None, ('expert', 'tensor')), may hold values from -0.09375 to 0.09375
- w_up: bfloat16 [4096, 65536], P(None, ('expert', 'tensor')), may hold values from -0.09375 to 0.09375
- w_down: bfloat16 [65536, 4096], P(('expert', 'tensor')), may hold values from -0.0625 to 0.0625
- expert_ids: int32 [512, 2], P(('groups', 'expert')), parts along dimension 0, may hold values from 0 to 7, all different within a row; in each aligned block of 64 rows (0 to 63, 64 to 127, ...) at most 32 rows name the same one
- gate_weights: float32 [512, 2], P(('groups', 'expert')), parts along dimension 0, may hold values from 0.1 to 1
Outputs:
- moe_out: bfloat16 [512, 4096], P(('groups', 'expert'), 'tensor'), parts along dimension 0
There are 2 independent parts, one for each index of `groups`. A program takes and returns all parts, laid end to end along the dimension named above; an argument that names none is the same for every part. Nothing has to cross between parts.
Inputs may be any that keep to these rules, and one draw needn't show every extreme that they name: `expert_ids`: each request names two different experts. Within the rows of one device (aligned blocks of 64 rows) no expert is named by more than 32 rows, and in some blocks one expert is named by exactly 32 rows.
All inputs are finite; a program needn't handle non-finite values.
Results may differ from a plain program's by a relative error of at most 0.008.
Values may be sent and summed in bfloat16 or wider, within the bound.
A program may use at most 192 MiB of HBM per device.

v0:
```python
import jax
import jax.numpy as jnp
from jax import lax
from jax.sharding import PartitionSpec as P

EXPERTS = 8


def lookup(targets, token_table, valid_table):
    select = (targets[..., None] == jnp.arange(token_table.shape[0], dtype=jnp.int32)).astype(
        jnp.int32
    )
    token_at = jnp.sum(select[..., None] * token_table, axis=-2)
    valid_at = jnp.sum(select[..., None] * valid_table, axis=-2)
    return (token_at, valid_at)


def pack_rows(normed, targets, token_table, valid_table):
    token_at, valid_at = lookup(targets, token_table, valid_table)
    picked = jnp.take(normed, token_at.reshape(-1), axis=0)
    picked = picked.reshape(token_at.shape + (normed.shape[1],))
    return picked * valid_at[..., None].astype(jnp.bfloat16)


def per_device(tokens, norm_gain, w_gate, w_up, w_down, expert_ids, gate_weights):
    n_expert = lax.axis_size("expert")
    n_tensor = lax.axis_size("tensor")
    tok_rows = tokens.shape[0]
    width_local = tokens.shape[1]
    width_full = width_local * n_tensor
    capacity = tok_rows // 2
    per_expert = n_expert * n_tensor // EXPERTS
    tensor_index = lax.axis_index("tensor")
    peers = jnp.arange(n_expert, dtype=jnp.int32)
    own_targets = ((peers * n_tensor + tensor_index) // per_expert)[:, None]
    flat_ids = expert_ids.reshape(-1)
    onehot = (flat_ids[:, None] == jnp.arange(EXPERTS, dtype=jnp.int32)[None, :]).astype(jnp.int32)
    running = jnp.cumsum(onehot, axis=0)
    slot_of = jnp.sum(running * onehot, axis=1) - 1
    pair_token = jnp.arange(flat_ids.shape[0], dtype=jnp.int32) // 2
    slot_hits = onehot[:, :, None] * (
        slot_of[:, None, None] == jnp.arange(capacity, dtype=jnp.int32)[None, None, :]
    ).astype(jnp.int32)
    token_table = jnp.sum(slot_hits * pair_token[:, None, None], axis=0)
    valid_table = jnp.sum(slot_hits, axis=0)
    full_rows = lax.all_gather(tokens, "tensor", axis=1, tiled=True)
    values = full_rows.astype(jnp.float32)
    sum_squares = jnp.sum(values * values, axis=1)
    scale = lax.rsqrt(sum_squares / width_full + 1e-05)
    normed = (values * scale[:, None] * norm_gain[None, :]).astype(jnp.bfloat16)
    outbound = pack_rows(normed, own_targets, token_table, valid_table)
    own_block = lax.all_to_all(outbound, "expert", split_axis=0, concat_axis=0, tiled=True)
    items = own_block.shape[2]
    flattened = own_block.reshape(-1, own_block.shape[3])
    gate_act = jnp.dot(flattened, w_gate, preferred_element_type=jnp.float32)
    up_act = jnp.dot(flattened, w_up, preferred_element_type=jnp.float32)
    hidden = (jax.nn.silu(gate_act) * up_act).astype(jnp.bfloat16)
    partial_value = jnp.dot(hidden, w_down, preferred_element_type=jnp.float32)
    partial_value = partial_value.reshape(n_expert, 1, items, partial_value.shape[1])
    returned = lax.all_to_all(partial_value, "expert", split_axis=0, concat_axis=0, tiled=True)
    mixing = (
        jnp.arange(EXPERTS, dtype=jnp.int32)[:, None] == own_targets.reshape(-1)[None, :]
    ).astype(jnp.float32)
    out_width = returned.shape[3]
    by_expert = jnp.dot(
        mixing,
        returned.reshape(own_targets.size, -1),
        precision=lax.Precision.HIGHEST,
        preferred_element_type=jnp.float32,
    )
    by_expert = by_expert.reshape(EXPERTS * capacity, out_width)
    picks = jnp.take(by_expert, flat_ids * capacity + slot_of, axis=0)
    mixed = jnp.sum(picks.reshape(tok_rows, 2, out_width) * gate_weights[:, :, None], axis=1)
    mixed = lax.psum_scatter(mixed, "tensor", scatter_dimension=1, tiled=True)
    return mixed.astype(jnp.bfloat16)


def solution(mesh):
    in_specs = (
        P(("groups", "expert"), "tensor"),
        P(),
        P(None, ("expert", "tensor")),
        P(None, ("expert", "tensor")),
        P(("expert", "tensor"), None),
        P(("groups", "expert"), None),
        P(("groups", "expert"), None),
    )
    out_specs = P(("groups", "expert"), "tensor")
    return jax.shard_map(
        per_device, mesh=mesh, in_specs=in_specs, out_specs=out_specs, check_vma=False
    )
```

profile of v0, /device:TPU:0, one launch (start us, length us, event | category | flops | bytes accessed | tf_op | source)
XLA Modules:
  0.0 173.0 jit_solution(17244527256869342859)
XLA Ops:
  6.5 0.8 copy.25
  7.3 0.1 reshape.291
  7.4 0.1 fusion.12
  7.6 0.2 reduce_window_sum.11
  7.8 0.2 select_reduce_fusion
  8.1 0.3 multiply_reduce_fusion.1
  8.4 0.1 multiply_reduce_fusion.2
  8.5 0.1 reshape.292
  8.6 17.6 %all_gather.3 = bf16[64,4096]{1,0:T(8,128)(2,1)S(1)} all-gather(bf16[64,1024]{1,0:T(8,128)(2,1)} %param.7), channel_id=1, replica_groups=mesh['groups'=2,'expert'=4,'tensor'=4] {'tensor'}, dimensions={1}, use_global_device_ids=true | all-gather | bytes 655360 | tf_op jit(solution)/shard_map/all_gather | solution.py:46
  26.2 0.2 fusion.7
  26.4 0.9 fusion.9
  27.4 1.2 gather_fusion
  28.6 0.2 select_multiply_fusion
  28.8 17.0 %all_to_all.10 = bf16[4,1,32,4096]{3,2,1,0:T(8,128)(2,1)S(1)} all-to-all(bf16[4,1,32,4096]{3,2,1,0:T(8,128)(2,1)S(1)} %select_multiply_fusion), channel_id=1, replica_groups=mesh['groups'=2,'expert'=4,'tensor'=4] {'expert'}, dimensions={0} | all-to-all | bytes 2097152 | tf_op jit(solution)/shard_map/all_to_all | solution.py:52
  45.7 12.9 %fusion.20 = f32[128,4096]{1,0:T(8,128)S(1)} fusion(bf16[128,4096]{1,0:T(8,128)(2,1)S(1)} %bitcast.26, bf16[4096,4096]{1,0:T(8,128)(2,1)} %param.9), kind=kOutput, calls=%fused_computation.56 | convolution fusion | flops 4294967296 | bytes 36700160 | tf_op jit(solution)/shard_map/dot_general | solution.py:55
  58.7 25.3 %fusion.1 = f32[128,4096]{1,0:T(8,128)} fusion(bf16[4096,4096]{1,0:T(8,128)(2,1)} %param.11, bf16[128,4096]{1,0:T(8,128)(2,1)S(1)} %bitcast.27, bf16[4096,4096]{1,0:T(8,128)(2,1)} %param.10, f32[128,4096]{1,0:T(8,128)S(1)} %fusion.20), kind=kOutput, calls=%fused_computation.4 | convolution fusion | flops 8593080320 | bytes 72351744 | tf_op jit(solution)/shard_map/dot_general | solution.py:58
  84.0 3.7 %all-to-all-start.1 = ((f32[4,1,32,4096]{3,2,1,0:T(8,128)}), f32[4,1,32,4096]{3,2,1,0:T(8,128)S(1)}, u32[]{:S(2)}, u32[]{:S(2)}) async-start(f32[4,1,32,4096]{3,2,1,0:T(8,128)} %bitcast.29), calls=%async_computation.1 | async-start | bytes 4194304 | tf_op jit(solution)/shard_map/all_to_all | solution.py:60
  87.8 0.2 reduce-scatter.2.cloned.1.call-start
  88.0 0.1 sub.19
  88.1 0.1 copy.31
  88.2 0.1 mul.167
  88.5 0.1 copy.27
  88.6 0.1 copy.32
  88.7 24.7 %all-to-all-done.1 = f32[4,1,32,4096]{3,2,1,0:T(8,128)S(1)} async-done(((f32[4,1,32,4096]{3,2,1,0:T(8,128)}), f32[4,1,32,4096]{3,2,1,0:T(8,128)S(1)}, u32[]{:S(2)}, u32[]{:S(2)}) %all-to-all-start.1) | async-done | bytes 2097184 | tf_op jit(solution)/shard_map/all_to_all | solution.py:60
  113.4 1.4 copy.33
  114.7 4.0 %fusion.14 = f32[8,131072]{1,0:T(8,128)} fusion(f32[4,131072]{1,0:T(4,128)S(1)} %bitcast.24, s32[4]{0:T(128)S(1)} %and_select_fusion.1), kind=kOutput, calls=%fused_computation.32 | convolution fusion | flops 50331680 | bytes 6291472 | tf_op jit(solution)/shard_map/dot_general | solution.py:65
  118.8 4.9 %reshape.296 = f32[256,4096]{1,0:T(8,128)} reshape(f32[8,131072]{1,0:T(8,128)} %fusion.14) | data formatting | bytes 8388608 | tf_op jit(solution)/shard_map/reshape | solution.py:71
  123.6 5.6 %gather_fusion.1 = f32[128,4096]{1,0:T(8,128)} fusion(f32[256,4096]{1,0:T(8,128)} %reshape.296, s32[1024]{0:T(1024)S(1)} %pad_clamp_fusion), kind=kCustom, calls=%fused_computation.1 | custom fusion | bytes 4194816 | tf_op jit(solution)/shard_map/jit(_take)/gather | solution.py:72
  129.3 2.5 %gather.15 = f32[64,2,4096]{2,1,0:T(2,128)S(1)} reshape(f32[128,4096]{1,0:T(8,128)} %gather_fusion.1) | data formatting | bytes 4194304 | tf_op jit(solution)/shard_map/jit(_take)/gather | solution.py:72
  131.8 4.5 %multiply_reduce_fusion = f32[64,4096]{1,0:T(8,128)} fusion(f32[64,2,4096]{2,1,0:T(2,128)S(1)} %gather.15, pred[64,2]{1,0:T(8,128)(4,1)S(1)} %copy.27, f32[64,2]{1,0:T(8,128)S(1)} %copy.32), kind=kLoop, calls=%fused_computation.5 | loop fusion | flops 1310720 | bytes 3146368 | tf_op jit(solution)/shard_map/reduce_sum | solution.py:73
  136.3 28.3 %reduce-scatter.2.cloned.1.call-done = f32[64,1024]{1,0:T(8,128)} async-done(((f32[64,4096]{1,0:T(8,128)}), f32[64,1024]{1,0:T(8,128)}) %reduce-scatter.2.cloned.1.call-update) | async-done | bytes 262160 | tf_op jit(solution)/shard_map/reduce_scatter | solution.py:74
  164.6 1.6 convert_element_type.52
  (21 shorter events, 0.3 us)
Async XLA Ops:
  84.0 4.1 %copy-start = (s32[64,2]{0,1:T(2,128)S(1)}, s32[64,2]{0,1:T(2,128)}, u32[]{:S(2)}) copy-start(s32[64,2]{0,1:T(2,128)} %param.12) | copy-start | bytes 1540
  84.0 4.6 %copy-start.1 = (f32[64,2]{0,1:T(2,128)S(1)}, f32[64,2]{0,1:T(2,128)}, u32[]{:S(2)}) copy-start(f32[64,2]{0,1:T(2,128)} %param.13) | copy-start | bytes 1540
  84.0 29.4 %all-to-all-start.1 = ((f32[4,1,32,4096]{3,2,1,0:T(8,128)}), f32[4,1,32,4096]{3,2,1,0:T(8,128)S(1)}, u32[]{:S(2)}, u32[]{:S(2)}) async-start(f32[4,1,32,4096]{3,2,1,0:T(8,128)} %bitcast.29), calls=%async_computation.1 | async-start | bytes 4194304 | tf_op jit(solution)/shard_map/all_to_all | solution.py:60
  87.8 76.8 %reduce-scatter.2.cloned.1.call-start = ((), (), s32[]{:S(2)}) async-start(), calls=%async_computation.3 | async-start | bytes 1310720 | tf_op jit(solution)/shard_map/reduce_scatter | solution.py:74
Sparse Core Ops, SparseCore 0:
  136.4 28.1 reduce-scatter.1
where the time goes:
time: 173 us
  waiting for transfers between devices  53 us (31%)
  matrix products  42.3 us (24%)
  blocking collectives  34.6 us (20%)
  local copies, waits for them, and re-layouts  17.2 us (10%)
  between operations  13.6 us (8%)
  other arithmetic  8.46 us (5%)
  starting transfers between devices  3.96 us (2%)
    reduce_scatter x1, waiting for transfers between devices, per_device(): mixed = lax.psum_scatter(mixed, 'tensor', scatter_dimension=1, tiled=True)  28.3 us
    dot_general x1, matrix products, per_device(): partial_value = jnp.dot(hidden, w_down, preferred_element_type=jnp.float32)  25.3 us
    all_to_all x1, waiting for transfers between devices, per_device(): lax.all_to_all(partial_value, 'expert', split_axis=0, concat_axis=0, tile...  24.7 us
    all_gather x1, blocking collectives, per_device(): full_rows = lax.all_gather(tokens, 'tensor', axis=1, tiled=True)  17.6 us
    all_to_all x1, blocking collectives, per_device(): lax.all_to_all(outbound, 'expert', split_axis=0, concat_axis=0, tiled=True)  17 us
    dot_general x1, matrix products, per_device(): gate_act = jnp.dot(flattened, w_gate, preferred_element_type=jnp.float32)  12.9 us
    gather x2, local copies, waits for them, and re-layouts, per_device(): picks = jnp.take(by_expert, flat_ids * capacity + slot_of, axis=0)  8.11 us
    reshape x1, local copies, waits for them, and re-layouts, per_device(): by_expert = by_expert.reshape(EXPERTS * capacity, out_width)  4.86 us
  transfers between devices with their start and end apart: 2, of which 2 were waited for; matrix products, arithmetic and copies ran while one was open for 0% of the time, Pallas kernels for 0%

commit v1 on v0

--- a/solution.py
+++ b/solution.py
@@ -4,6 +4,16 @@
 from jax.sharding import PartitionSpec as P
 
 EXPERTS = 8
+
+
+def turned_line(block, axis, dim):
+    peers = lax.axis_size(axis)
+    held, parts = (block, [block])
+    for _ in range(peers - 1):
+        held = lax.ppermute(held, axis, [(i, (i + 1) % peers) for i in range(peers)])
+        parts.insert(0, held)
+    line = jnp.concatenate(parts, axis=dim)
+    return jnp.roll(line, (lax.axis_index(axis) + 1) * block.shape[dim], axis=dim)
 
 
 def lookup(targets, token_table, valid_table):
@@ -43,7 +53,7 @@
     ).astype(jnp.int32)
     token_table = jnp.sum(slot_hits * pair_token[:, None, None], axis=0)
     valid_table = jnp.sum(slot_hits, axis=0)
-    full_rows = lax.all_gather(tokens, "tensor", axis=1, tiled=True)
+    full_rows = turned_line(tokens, "tensor", 1)
     values = full_rows.astype(jnp.float32)
     sum_squares = jnp.sum(values * values, axis=1)
     scale = lax.rsqrt(sum_squares / width_full + 1e-05)

time: 173 us -> 173 us (level)
  blocking collectives: 34.6 us -> 17 us
  waiting for transfers between devices: 53 us -> 66 us
  starting transfers between devices: 3.96 us -> 7.02 us
    all_gather x1 -> x0, blocking collectives: 17.6 us -> none  [per_device(): full_rows = lax.all_gather(tokens, 'tensor', axis=1, tiled=True)]
    ppermute x0 -> x3, waiting for transfers between devices: none -> 16.3 us  [turned_line(): lax.ppermute(held, axis, [(i, (i + 1) % peers) for i in range(peers)])]
    reduce_scatter x1, waiting for transfers between devices: 28.3 us -> 24.7 us  [per_device(): mixed = lax.psum_scatter(mixed, 'tensor', scatter_dimension=1, tiled=True)]
    ppermute x0 -> x3, starting transfers between devices: none -> 3.06 us  [turned_line(): lax.ppermute(held, axis, [(i, (i + 1) % peers) for i in range(peers)])]
  transfers between devices with their start and end apart: 2 -> 5, of which waited for: 2 -> 5; matrix products, arithmetic and copies ran while one was open for 0% -> 2% of each run, Pallas kernels for 0% -> 0%
where the time goes in v1:
time: 173 us
  waiting for transfers between devices  66 us (38%)
  matrix products  42.3 us (24%)
  local copies, waits for them, and re-layouts  18.2 us (11%)
  blocking collectives  17 us (10%)
  between operations  13.6 us (8%)
  other arithmetic  8.43 us (5%)
  starting transfers between devices  7.02 us (4%)
    dot_general x1, matrix products, per_device(): partial_value = jnp.dot(hidden, w_down, preferred_element_type=jnp.float32)  25.3 us
    all_to_all x1, waiting for transfers between devices, per_device(): lax.all_to_all(partial_value, 'expert', split_axis=0, concat_axis=0, tile...  24.9 us
    reduce_scatter x1, waiting for transfers between devices, per_device(): mixed = lax.psum_scatter(mixed, 'tensor', scatter_dimension=1, tiled=True)  24.7 us
    all_to_all x1, blocking collectives, per_device(): lax.all_to_all(outbound, 'expert', split_axis=0, concat_axis=0, tiled=True)  17 us
    ppermute x3, waiting for transfers between devices, turned_line(): lax.ppermute(held, axis, [(i, (i + 1) % peers) for i in range(peers)])  16.3 us
    dot_general x1, matrix products, per_device(): gate_act = jnp.dot(flattened, w_gate, preferred_element_type=jnp.float32)  12.9 us
    gather x2, local copies, waits for them, and re-layouts, per_device(): picks = jnp.take(by_expert, flat_ids * capacity + slot_of, axis=0)  8.11 us
    reshape x1, local copies, waits for them, and re-layouts, per_device(): by_expert = by_expert.reshape(EXPERTS * capacity, out_width)  4.86 us
  transfers between devices with their start and end apart: 5, of which 5 were waited for; matrix products, arithmetic and copies ran while one was open for 2% of the time, Pallas kernels for 0%

profile of v1, /device:TPU:0, one launch (start us, length us, event | category | flops | bytes accessed | tf_op | source)
XLA Modules:
  0.0 172.5 jit_solution(6577529786523449463)
XLA Ops:
  6.5 3.1 %collective-permute-start = (bf16[64,1024]{1,0:T(8,128)(2,1)}, bf16[64,1024]{1,0:T(8,128)(2,1)S(1)}, u32[]{:S(2)}, u32[]{:S(2)}) collective-permute-start(bf16[64,1024]{1,0:T(8,128)(2,1)} %param.7), channel_id=1, source_target_pairs={{0,1},{1,2},{2,3},{3,0},{4,5},{5,6},{6,7},{7,4},{8,9},{9,10},{10,1... | collective-permute-start | bytes 393224 | tf_op jit(solution)/shard_map/ppermute | solution.py:13
  9.6 0.8 copy.25
  10.4 0.7 broadcast_multiply_fusion
  11.0 0.1 reshape.291
  11.3 0.2 reduce_window_sum.11
  11.5 0.2 select_reduce_fusion
  11.8 0.3 multiply_reduce_fusion.1
  12.4 0.1 mul.171
  12.6 2.8 %collective-permute-done = bf16[64,1024]{1,0:T(8,128)(2,1)S(1)} collective-permute-done((bf16[64,1024]{1,0:T(8,128)(2,1)}, bf16[64,1024]{1,0:T(8,128)(2,1)S(1)}, u32[]{:S(2)}, u32[]{:S(2)}) %collective-permute-start) | collective-permute-done | bytes 131104 | tf_op jit(solution)/shard_map/ppermute | solution.py:13
  15.4 6.8 %collective-permute-done.1 = bf16[64,1024]{1,0:T(8,128)(2,1)S(1)} collective-permute-done((bf16[64,1024]{1,0:T(8,128)(2,1)S(1)}, bf16[64,1024]{1,0:T(8,128)(2,1)S(1)}, u32[]{:S(2)}, u32[]{:S(2)}) %collective-permute-start.1) | collective-permute-done | bytes 131104 | tf_op jit(solution)/shard_map/ppermute | solution.py:13
  22.2 6.7 %collective-permute-done.2 = bf16[64,1024]{1,0:T(8,128)(2,1)S(1)} collective-permute-done((bf16[64,1024]{1,0:T(8,128)(2,1)S(1)}, bf16[64,1024]{1,0:T(8,128)(2,1)S(1)}, u32[]{:S(2)}, u32[]{:S(2)}) %collective-permute-start.2) | collective-permute-done | bytes 131104 | tf_op jit(solution)/shard_map/ppermute | solution.py:13
  29.0 0.9 constant_dynamic-update-slice_fusion.4
  30.0 0.2 fusion.7
  30.2 0.2 fusion.9
  30.4 1.2 gather_fusion
  31.6 0.2 select_multiply_fusion
  31.8 17.0 %all_to_all.10 = bf16[4,1,32,4096]{3,2,1,0:T(8,128)(2,1)S(1)} all-to-all(bf16[4,1,32,4096]{3,2,1,0:T(8,128)(2,1)S(1)} %select_multiply_fusion), channel_id=1, replica_groups=mesh['groups'=2,'expert'=4,'tensor'=4] {'expert'}, dimensions={0} | all-to-all | bytes 2097152 | tf_op jit(solution)/shard_map/all_to_all | solution.py:62
  48.8 12.9 %fusion.20 = f32[128,4096]{1,0:T(8,128)S(1)} fusion(bf16[128,4096]{1,0:T(8,128)(2,1)S(1)} %bitcast.26, bf16[4096,4096]{1,0:T(8,128)(2,1)} %param.9), kind=kOutput, calls=%fused_computation.64 | convolution fusion | flops 4294967296 | bytes 36700160 | tf_op jit(solution)/shard_map/dot_general | solution.py:65
  61.7 25.3 %fusion.1 = f32[128,4096]{1,0:T(8,128)} fusion(bf16[4096,4096]{1,0:T(8,128)(2,1)} %param.11, bf16[128,4096]{1,0:T(8,128)(2,1)S(1)} %bitcast.27, bf16[4096,4096]{1,0:T(8,128)(2,1)} %param.10, f32[128,4096]{1,0:T(8,128)S(1)} %fusion.20), kind=kOutput, calls=%fused_computation.4 | convolution fusion | flops 8593080320 | bytes 72351744 | tf_op jit(solution)/shard_map/dot_general | solution.py:68
  87.1 3.7 %all-to-all-start.1 = ((f32[4,1,32,4096]{3,2,1,0:T(8,128)}), f32[4,1,32,4096]{3,2,1,0:T(8,128)S(1)}, u32[]{:S(2)}, u32[]{:S(2)}) async-start(f32[4,1,32,4096]{3,2,1,0:T(8,128)} %bitcast.29), calls=%async_computation.1 | async-start | bytes 4194304 | tf_op jit(solution)/shard_map/all_to_all | solution.py:70
  90.8 0.2 reduce-scatter.2.cloned.1.call-start
  91.0 0.1 sub.23
  91.3 0.1 copy.27
  91.5 24.9 %all-to-all-done.1 = f32[4,1,32,4096]{3,2,1,0:T(8,128)S(1)} async-done(((f32[4,1,32,4096]{3,2,1,0:T(8,128)}), f32[4,1,32,4096]{3,2,1,0:T(8,128)S(1)}, u32[]{:S(2)}, u32[]{:S(2)}) %all-to-all-start.1) | async-done | bytes 2097184 | tf_op jit(solution)/shard_map/all_to_all | solution.py:70
  116.4 1.4 copy.33
  117.8 4.0 %fusion.14 = f32[8,131072]{1,0:T(8,128)} fusion(f32[4,131072]{1,0:T(4,128)S(1)} %bitcast.24, s32[4]{0:T(128)S(1)} %and_select_fusion.1), kind=kOutput, calls=%fused_computation.40 | convolution fusion | flops 50331680 | bytes 6291472 | tf_op jit(solution)/shard_map/dot_general | solution.py:75
  121.8 4.9 %reshape.296 = f32[256,4096]{1,0:T(8,128)} reshape(f32[8,131072]{1,0:T(8,128)} %fusion.14) | data formatting | bytes 8388608 | tf_op jit(solution)/shard_map/reshape | solution.py:81
  126.7 5.6 %gather_fusion.1 = f32[128,4096]{1,0:T(8,128)} fusion(f32[256,4096]{1,0:T(8,128)} %reshape.296, s32[1024]{0:T(1024)S(1)} %get-tuple-element.9), kind=kCustom, calls=%fused_computation.1 | custom fusion | bytes 4194816 | tf_op jit(solution)/shard_map/jit(_take)/gather | solution.py:82
  132.3 2.5 %gather.15 = f32[64,2,4096]{2,1,0:T(2,128)S(1)} reshape(f32[128,4096]{1,0:T(8,128)} %gather_fusion.1) | data formatting | bytes 4194304 | tf_op jit(solution)/shard_map/jit(_take)/gather | solution.py:82
  134.8 4.5 %multiply_reduce_fusion = f32[64,4096]{1,0:T(8,128)} fusion(f32[64,2,4096]{2,1,0:T(2,128)S(1)} %gather.15, pred[64,2]{1,0:T(8,128)(4,1)S(1)} %copy.27, f32[64,2]{1,0:T(8,128)S(1)} %copy.32), kind=kLoop, calls=%fused_computation.5 | loop fusion | flops 1310720 | bytes 3146368 | tf_op jit(solution)/shard_map/reduce_sum | solution.py:83
  139.3 24.7 %reduce-scatter.2.cloned.1.call-done = f32[64,1024]{1,0:T(8,128)} async-done(((f32[64,4096]{1,0:T(8,128)}), f32[64,1024]{1,0:T(8,128)}) %reduce-scatter.2.cloned.1.call-update) | async-done | bytes 262160 | tf_op jit(solution)/shard_map/reduce_scatter | solution.py:84
  164.0 1.6 convert_element_type.52
  (37 shorter events, 0.8 us)
Async XLA Ops:
  6.5 23.4 %copy-start = (bf16[64,1024]{1,0:T(8,128)(2,1)S(1)}, bf16[64,1024]{1,0:T(8,128)(2,1)}, u32[]{:S(2)}) copy-start(bf16[64,1024]{1,0:T(8,128)(2,1)} %param.7) | copy-start | bytes 393220
  6.5 23.7 %copy-start.1 = (f32[4096]{0:T(1024)S(1)}, f32[4096]{0:T(1024)}, u32[]{:S(2)}) copy-start(f32[4096]{0:T(1024)} %param.8) | copy-start | bytes 49156
  6.5 8.9 %collective-permute-start = (bf16[64,1024]{1,0:T(8,128)(2,1)}, bf16[64,1024]{1,0:T(8,128)(2,1)S(1)}, u32[]{:S(2)}, u32[]{:S(2)}) collective-permute-start(bf16[64,1024]{1,0:T(8,128)(2,1)} %param.7), channel_id=1, source_target_pairs={{0,1},{1,2},{2,3},{3,0},{4,5},{5,6},{6,7},{7,4},{8,9},{9,10},{10,1... | collective-permute-start | bytes 393224 | tf_op jit(solution)/shard_map/ppermute | solution.py:13
  15.4 6.8 %collective-permute-start.1 = (bf16[64,1024]{1,0:T(8,128)(2,1)S(1)}, bf16[64,1024]{1,0:T(8,128)(2,1)S(1)}, u32[]{:S(2)}, u32[]{:S(2)}) collective-permute-start(bf16[64,1024]{1,0:T(8,128)(2,1)S(1)} %collective-permute-done), channel_id=1, source_target_pairs={{0,1},{1,2},{2,3},{3,0},{4,5},{5,6},{6,7},{7,4},{8,9},{9,10},{10,1... | collective-permute-start | bytes 393224 | tf_op jit(solution)/shard_map/ppermute | solution.py:13
  22.2 6.8 %collective-permute-start.2 = (bf16[64,1024]{1,0:T(8,128)(2,1)S(1)}, bf16[64,1024]{1,0:T(8,128)(2,1)S(1)}, u32[]{:S(2)}, u32[]{:S(2)}) collective-permute-start(bf16[64,1024]{1,0:T(8,128)(2,1)S(1)} %collective-permute-done.1), channel_id=1, source_target_pairs={{0,1},{1,2},{2,3},{3,0},{4,5},{5,6},{6,7},{7,4},{8,9},{9,10},{10,1... | collective-permute-start | bytes 393224 | tf_op jit(solution)/shard_map/ppermute | solution.py:13
  87.0 4.2 %copy-start.2 = (s32[64,2]{0,1:T(2,128)S(1)}, s32[64,2]{0,1:T(2,128)}, u32[]{:S(2)}) copy-start(s32[64,2]{0,1:T(2,128)} %param.12) | copy-start | bytes 1540
  87.0 4.3 %copy-start.3 = (f32[64,2]{0,1:T(2,128)S(1)}, f32[64,2]{0,1:T(2,128)}, u32[]{:S(2)}) copy-start(f32[64,2]{0,1:T(2,128)} %param.13) | copy-start | bytes 1540
  87.1 29.4 %all-to-all-start.1 = ((f32[4,1,32,4096]{3,2,1,0:T(8,128)}), f32[4,1,32,4096]{3,2,1,0:T(8,128)S(1)}, u32[]{:S(2)}, u32[]{:S(2)}) async-start(f32[4,1,32,4096]{3,2,1,0:T(8,128)} %bitcast.29), calls=%async_computation.1 | async-start | bytes 4194304 | tf_op jit(solution)/shard_map/all_to_all | solution.py:70
  90.8 73.2 %reduce-scatter.2.cloned.1.call-start = ((), (), s32[]{:S(2)}) async-start(), calls=%async_computation.3 | async-start | bytes 1310720 | tf_op jit(solution)/shard_map/reduce_scatter | solution.py:84
Sparse Core Ops, SparseCore 0:
  139.4 24.5 reduce-scatter.1
